TPU v7x, 32 devices: a whole 2x2x4 slice. The times are simulated.
32 devices in a mesh: grp: 2 (over x), seq: 16 (over z, y, core).
Axes of the slice: x: 2, y: 2, z: 4, core: 2. Of those that a mesh axis runs over, the one named last changes fastest.
Arguments:
- llm_grad: bfloat16 [4096, 8192], P('seq', 'grp'), may hold values from -6 to 6
- image_grid: int32 [256, 2], replicated, may hold values from 1 to 3, as said below
- image_owner: int32 [256], replicated, may hold values from 0 to 15, as said below
- row_start: int32 [256], replicated, may hold values from 0 to 255, as said below
- merger_pre: bfloat16 [48, 16, 2560], P(None, 'seq', 'grp'), may hold values from -6 to 6
- vit_out: bfloat16 [192, 16, 1280], P(None, 'seq'), may hold values from -6 to 6
- vit_pre: bfloat16 [192, 16, 2560], P(None, 'seq', 'grp'), may hold values from -6 to 6
- ln_gain: float32 [1280], replicated, may hold values from 0.25 to 1.75
- merger_out_w: bfloat16 [8192, 2560], P('seq', 'grp'), may hold values from -0.0625 to 0.0625
- merger_in_w: bfloat16 [2560, 5120], P('grp', 'seq'), may hold values from -0.125 to 0.125
- vit_fc2_w: bfloat16 [1280, 2560], P('seq', 'grp'), may hold values from -0.15625 to 0.15625
Outputs:
- patch_grad: bfloat16 [192, 16, 1280], P('grp', 'seq')
- fc1_grad: bfloat16 [192, 16, 2560], P(None, 'seq', 'grp')
- fc2_w_grad: float32 [1280, 2560], P('seq', 'grp')
Inputs may be any that keep to these rules, and one draw needn't show every extreme that they name: `image_grid`: height times width is 1 to 3; the first image of every shard is 1 by 3; the last image of shard 0 is 1 by 1. `image_owner`: the 16 images of one shard have 16 different owners. An image's rows row_start to row_start + t - 1 lie inside its shard and meet no other image's rows; a shard's images follow the order of k; the last image of every shard ends at the shard's last row; the first image of shard 0 starts at row 0.
All inputs are finite; a program needn't handle non-finite values.
Results may differ from a plain program's by a relative error of at most 0.02.
Values may be sent and summed in bfloat16 or wider, within the bound.
A program may use at most 128 MiB of HBM per device.

v0:
```python
import jax
import jax.numpy as jnp
from jax import lax
from jax.sharding import PartitionSpec as P

SLOT = 3


def gelu_slope(values):
    return (
        0.5 * (1.0 + lax.erf(values * 0.7071067811865476))
        + values * jnp.exp(-0.5 * values * values) * 0.3989422804014327
    )


def patch_table(widths, counts, slots):
    places = jnp.arange(4 * slots, dtype=jnp.int32)
    merged = places // 4
    corner = places % 4
    row_in = merged[None, :] // widths[:, None]
    col_in = merged[None, :] % widths[:, None]
    target = (
        (2 * row_in + corner[None, :] // 2) * (2 * widths[:, None])
        + 2 * col_in
        + corner[None, :] % 2
    )
    usable = merged[None, :] < counts[:, None]
    return ((target[:, None, :] == places[None, :, None]) & usable[:, None, :]).astype(jnp.float32)


def norm_backward(upstream, inputs, scales):
    average = jnp.mean(inputs, -1, keepdims=True)
    centred = inputs - average
    inverse_std = lax.rsqrt(jnp.mean(centred * centred, -1, keepdims=True) + 1e-06)
    normed = centred * inverse_std
    scaled = upstream * scales
    return inverse_std * (
        scaled
        - jnp.mean(scaled, -1, keepdims=True)
        - normed * jnp.mean(scaled * normed, -1, keepdims=True)
    )


def on_device(
    llm_grad,
    image_grid,
    image_owner,
    row_start,
    merger_pre,
    vit_out,
    vit_pre,
    ln_gain,
    merger_out_w,
    merger_in_w,
    vit_fc2_w,
):
    seq_count = lax.axis_size("seq")
    own_index = lax.axis_index("seq")
    grids = image_grid.reshape(seq_count, seq_count, 2)
    counts = grids[:, :, 0] * grids[:, :, 1]
    widths = grids[:, :, 1]
    owners = image_owner.reshape(seq_count, seq_count)
    starts = row_start.reshape(seq_count, seq_count)
    within = jnp.arange(SLOT, dtype=jnp.int32)
    peers = jnp.arange(seq_count, dtype=jnp.int32)
    shard_rows = llm_grad.shape[0]
    my_owners = lax.dynamic_index_in_dim(owners, own_index, 0, keepdims=False)
    my_counts = lax.dynamic_index_in_dim(counts, own_index, 0, keepdims=False)
    my_starts = lax.dynamic_index_in_dim(starts, own_index, 0, keepdims=False)
    targets = (my_owners[None, :] == peers[:, None]).astype(jnp.int32)
    send_counts = jnp.sum(targets * my_counts[None, :], 1)
    send_starts = jnp.sum(targets * my_starts[None, :], 1)
    indices = jnp.minimum(send_starts[:, None] + within[None, :], shard_rows - 1)
    usable = within[None, :] < send_counts[:, None]
    picked = jnp.take(llm_grad, indices.reshape(-1), axis=0)
    outgoing = jnp.where(usable.reshape(-1, 1), picked, jnp.zeros_like(picked)).reshape(
        seq_count, SLOT, llm_grad.shape[1]
    )
    received = (owners == own_index).astype(jnp.int32)
    recv_counts = jnp.sum(received * counts, 1)
    recv_widths = jnp.sum(received * widths, 1)
    wide_rows = lax.all_gather(outgoing.reshape(-1, llm_grad.shape[1]), "grp", axis=1, tiled=True)
    sliced = lax.all_to_all(wide_rows, "seq", split_axis=1, concat_axis=0, tiled=True)
    features = sliced.shape[1]
    by_owner = jnp.swapaxes(sliced.reshape(seq_count, seq_count, SLOT, features), 0, 1).reshape(
        -1, features
    )
    folded = jnp.dot(by_owner, merger_out_w, preferred_element_type=jnp.float32)
    arrived = lax.all_to_all(
        folded.astype(jnp.bfloat16), "seq", split_axis=0, concat_axis=0, tiled=True
    )
    unit_grad = jnp.sum(
        arrived.reshape(seq_count, seq_count * SLOT, -1).astype(jnp.float32), 0
    ).astype(jnp.bfloat16)
    pre_act = merger_pre[:, 0, :].astype(jnp.float32)
    pre_grad = (gelu_slope(pre_act) * unit_grad.astype(jnp.float32)).astype(jnp.bfloat16)
    all_pre = lax.all_gather(pre_grad, "seq", axis=0, tiled=True)
    part_cols = jnp.dot(all_pre, merger_in_w, preferred_element_type=jnp.float32)
    part_rows = lax.all_to_all(
        part_cols.astype(jnp.bfloat16), "seq", split_axis=0, concat_axis=1, tiled=True
    )
    merged_part = jnp.sum(lax.all_gather(part_rows, "grp", axis=0).astype(jnp.float32), 0)
    vit_width = vit_out.shape[2]
    table = patch_table(recv_widths, recv_counts, SLOT)
    patch_in = jnp.einsum(
        "spq,sqc->spc",
        table,
        merged_part.reshape(seq_count, 4 * SLOT, vit_width),
        precision=lax.Precision.HIGHEST,
    ).reshape(-1, vit_width)
    patch_grad = norm_backward(patch_in, vit_out[:, 0, :].astype(jnp.float32), ln_gain).astype(
        jnp.bfloat16
    )
    group_rows = patch_grad.shape[0] // lax.axis_size("grp")
    own_rows = lax.dynamic_slice_in_dim(
        patch_grad, lax.axis_index("grp") * group_rows, group_rows, 0
    )
    columns = patch_grad
    act_grad = jnp.dot(
        columns,
        lax.all_gather(vit_fc2_w, "seq", axis=0, tiled=True),
        preferred_element_type=jnp.float32,
    )
    fc_in = vit_pre[:, 0, :].astype(jnp.float32)
    sigmoid_q = jax.nn.sigmoid(1.702 * fc_in)
    activation = (fc_in * sigmoid_q).astype(jnp.bfloat16)
    fc1_grad = ((sigmoid_q + 1.702 * fc_in * sigmoid_q * (1.0 - sigmoid_q)) * act_grad).astype(
        jnp.bfloat16
    )
    columns = patch_grad
    weight_part = lax.dot_general(
        columns, activation, (((0,), (0,)), ((), ())), preferred_element_type=jnp.float32
    )
    weight_parts = lax.all_to_all(
        weight_part.astype(jnp.bfloat16), "seq", split_axis=0, concat_axis=0, tiled=True
    )
    weight_grad = jnp.sum(
        weight_parts.reshape(seq_count, -1, weight_part.shape[1]).astype(jnp.float32), 0
    )
    return (
        own_rows.reshape(group_rows, 1, vit_width),
        fc1_grad.reshape(-1, 1, vit_pre.shape[2]),
        weight_grad,
    )


def solution(mesh):
    return jax.shard_map(
        on_device,
        mesh=mesh,
        in_specs=(
            P("seq", "grp"),
            P(),
            P(),
            P(),
            P(None, "seq", "grp"),
            P(None, "seq", None),
            P(None, "seq", "grp"),
            P(),
            P("seq", "grp"),
            P("grp", "seq"),
            P("seq", "grp"),
        ),
        out_specs=(P("grp", "seq", None), P(None, "seq", "grp"), P("seq", "grp")),
        check_vma=False,
    )
```

profile of v0, /device:TPU:13, one launch (start us, length us, event | category | flops | bytes accessed | tf_op | source)
XLA Modules:
  0.0 296.6 jit_solution(5290898509459888009)
XLA Ops:
  7.2 0.9 reshape.493
  8.9 0.8 reshape.494
  10.4 0.8 gather_fusion
  11.3 10.7 %all_gather.15 = bf16[48,8192]{1,0:T(8,128)(2,1)S(1)} all-gather(bf16[48,4096]{1,0:T(8,128)(2,1)S(1)} %select_select_fusion), channel_id=1, replica_groups=mesh['grp'=2,'seq'=16] {'grp'}, dimensions={1}, use_global_device_ids=true | all-gather | bytes 1179648 | tf_op jit(solution)/shard_map/all_gather | solution.py:82
  22.1 26.4 %all_to_all.50 = bf16[48,16,512]{2,0,1:T(8,128)(2,1)S(1)} all-to-all(bf16[48,16,512]{2,0,1:T(8,128)(2,1)S(1)} %bitcast.84), channel_id=1, replica_groups=mesh['grp'=2,'seq'=16] {'seq'}, dimensions={1} | all-to-all | bytes 1572864 | tf_op jit(solution)/shard_map/all_to_all | solution.py:83
  49.6 1.4 reshape.497
  51.0 2.7 convolution_convert_fusion.1
  53.7 49.2 %all_to_all.51 = bf16[16,48,1280]{2,1,0:T(8,128)(2,1)} all-to-all(bf16[16,48,1280]{2,1,0:T(8,128)(2,1)S(1)} %bitcast.85), channel_id=1, replica_groups=mesh['grp'=2,'seq'=16] {'seq'}, dimensions={0} | all-to-all | bytes 3932160 | tf_op jit(solution)/shard_map/all_to_all | solution.py:89
  103.0 1.9 reduce_sum.108
  104.9 0.8 fusion.26
  106.9 38.0 %all-gather.3.cloned.1.call-done = bf16[768,1280]{1,0:T(8,128)(2,1)} async-done(((bf16[48,1280]{1,0:T(8,128)(2,1)}), bf16[768,1280]{1,0:T(8,128)(2,1)}) %all-gather.3.cloned.1.call-update) | async-done | bytes 1966096 | tf_op jit(solution)/shard_map/all_gather | solution.py:97
  144.9 2.6 convolution_convert_fusion.2
  147.5 1.1 copy.22
  148.5 6.4 %all-to-all-start.2 = ((bf16[16,48,320]{2,1,0:T(8,128)(2,1)}), bf16[16,48,320]{2,1,0:T(8,128)(2,1)}, u32[]{:S(2)}, u32[]{:S(2)}) async-start(bf16[16,48,320]{2,1,0:T(8,128)(2,1)} %bitcast.13), calls=%async_computation.2 | async-start | bytes 1179648 | tf_op jit(solution)/shard_map/all_to_all | solution.py:99
  155.0 1.1 reshape.503
  156.6 20.1 %all-to-all-done.2 = bf16[16,48,320]{2,1,0:T(8,128)(2,1)} async-done(((bf16[16,48,320]{2,1,0:T(8,128)(2,1)}), bf16[16,48,320]{2,1,0:T(8,128)(2,1)}, u32[]{:S(2)}, u32[]{:S(2)}) %all-to-all-start.2) | async-done | bytes 491552 | tf_op jit(solution)/shard_map/all_to_all | solution.py:99
  176.7 2.0 copy.23
  178.7 2.3 all_gather.17
  181.0 13.6 %all_gather.18 = bf16[2,48,5120]{2,1,0:T(8,128)(2,1)S(1)} all-gather(bf16[1,48,5120]{2,1,0:T(8,128)(2,1)} %all_gather.17), channel_id=1, replica_groups=mesh['grp'=2,'seq'=16] {'grp'}, dimensions={0}, use_global_device_ids=true | all-gather | bytes 1474560 | tf_op jit(solution)/shard_map/all_gather | solution.py:102
  194.6 1.1 convert_reduce_fusion.1
  195.8 2.5 reshape.498
  198.3 2.4 multiply_reduce_fusion.1
  200.8 1.1 copy-done.1
  201.8 1.3 multiply_convert_fusion
  203.1 1.2 convert_element_type.82
  204.3 3.9 %convolution_convert_fusion = bf16[1280,1280]{1,0:T(8,128)(2,1)} fusion(bf16[192,1280]{1,0:T(8,128)(2,1)S(1)} %convert_element_type.82, bf16[192,1,1280]{2,0,1:T(8,128)(2,1)} %param.17), kind=kOutput, calls=%fused_computation.1 | convolution fusion | flops 632504320 | bytes 4259840 | tf_op jit(solution)/shard_map/dot_general | solution.py:131
  208.1 5.6 %all-to-all-start.3 = ((bf16[16,80,1280]{2,1,0:T(8,128)(2,1)}), bf16[16,80,1280]{2,1,0:T(8,128)(2,1)}, u32[]{:S(2)}, u32[]{:S(2)}) async-start(bf16[16,80,1280]{2,1,0:T(8,128)(2,1)} %bitcast.81), calls=%async_computation.3 | async-start | bytes 6553600 | tf_op jit(solution)/shard_map/all_to_all | solution.py:134
  213.9 1.1 reshape.499
  215.0 1.7 multiply_convert_fusion.1
  217.5 3.6 %fusion.1 = bf16[192,1,1280]{2,0,1:T(8,128)(2,1)} fusion(bf16[192,1280]{1,0:T(8,128)(2,1)S(1)} %multiply_convert_fusion.1, bf16[1280,1280]{1,0:T(8,128)(2,1)} %all-gather.5.cloned.1.call-done, bf16[192,1,1280]{2,0,1:T(8,128)(2,1)S(1)} %copy-done.6), kind=kOutput, calls=%fused_computation.6 | convolution fusion | flops 631848960 | bytes 4751360 | tf_op jit(solution)/shard_map/dot_general | solution.py:119
  221.1 65.5 %all-to-all-done.3 = bf16[16,80,1280]{2,1,0:T(8,128)(2,1)} async-done(((bf16[16,80,1280]{2,1,0:T(8,128)(2,1)}), bf16[16,80,1280]{2,1,0:T(8,128)(2,1)}, u32[]{:S(2)}, u32[]{:S(2)}) %all-to-all-start.3) | async-done | bytes 3276832 | tf_op jit(solution)/shard_map/all_to_all | solution.py:134
  286.6 3.2 %convert_reduce_fusion = f32[80,1280]{1,0:T(8,128)} fusion(bf16[16,80,1280]{2,1,0:T(8,128)(2,1)} %all-to-all-done.3), kind=kLoop, calls=%fused_computation.2 | loop fusion | flops 3174400 | bytes 3686400 | tf_op jit(solution)/shard_map/reduce_sum | solution.py:137
  (52 shorter events, 5.4 us)
Async XLA Ops:
  7.2 3.2 %copy-start = (bf16[256,4096]{1,0:T(8,128)(2,1)S(1)}, bf16[256,4096]{1,0:T(8,128)(2,1)}, u32[]{:S(2)}) copy-start(bf16[256,4096]{1,0:T(8,128)(2,1)} %param.11) | copy-start | bytes 6291460
  7.2 137.7 %all-gather.3.cloned.1.call-start = ((), (), s32[]{:S(2)}) async-start(), calls=%async_computation.4 | async-start | bytes 2088960 | tf_op jit(solution)/shard_map/all_gather | solution.py:97
  103.0 1.9 copy-start.4
  103.0 3.5 %copy-start.3 = (bf16[192,1,1280]{2,0,1:T(8,128)(2,1)S(1)}, bf16[192,1,1280]{2,0,1:T(8,128)(2,1)}, u32[]{:S(2)}) copy-start(bf16[192,1,1280]{2,0,1:T(8,128)(2,1)} %param.16) | copy-start | bytes 1474564
  105.7 111.8 %all-gather.5.cloned.1.call-start = ((), (), s32[]{:S(2)}) async-start(), calls=%async_computation.5 | async-start | bytes 3481600 | tf_op jit(solution)/shard_map/all_gather | solution.py:121
  148.5 28.2 %all-to-all-start.2 = ((bf16[16,48,320]{2,1,0:T(8,128)(2,1)}), bf16[16,48,320]{2,1,0:T(8,128)(2,1)}, u32[]{:S(2)}, u32[]{:S(2)}) async-start(bf16[16,48,320]{2,1,0:T(8,128)(2,1)} %bitcast.13), calls=%async_computation.2 | async-start | bytes 1179648 | tf_op jit(solution)/shard_map/all_to_all | solution.py:99
  195.8 2.6 copy-start.5
  200.7 1.1 copy-start.1
  208.1 5.7 %copy-start.2 = (f32[16,12,1280]{2,1,0:T(8,128)S(1)}, f32[16,12,1280]{2,1,0:T(8,128)}, u32[]{:S(2)}) copy-start(f32[16,12,1280]{2,1,0:T(8,128)} %copy-done.1) | copy-start | bytes 2949124
  208.1 78.4 %all-to-all-start.3 = ((bf16[16,80,1280]{2,1,0:T(8,128)(2,1)}), bf16[16,80,1280]{2,1,0:T(8,128)(2,1)}, u32[]{:S(2)}, u32[]{:S(2)}) async-start(bf16[16,80,1280]{2,1,0:T(8,128)(2,1)} %bitcast.81), calls=%async_computation.3 | async-start | bytes 6553600 | tf_op jit(solution)/shard_map/all_to_all | solution.py:134
  215.0 2.5 copy-start.6
Sparse Core Ops, SparseCore 0:
  105.8 39.0 all-gather.2
  147.2 52.0 all-gather.4
where the time goes:
time: 298 us; the launch traced here: 297 us
  waiting for transfers between devices  124 us (42%)
  blocking collectives  99.9 us (34%)
  local copies, waits for them, and re-layouts  19.6 us (7%)
  matrix products  15.2 us (5%)
  between operations  14.3 us (5%)
  starting transfers between devices  12.2 us (4%)
  other arithmetic  11.3 us (4%)
    all_to_all x1, waiting for transfers between devices, on_device(): lax.all_to_all(weight_part.astype(jnp.bfloat16), 'seq', split_axis=0, con...  65.5 us
    all_to_all x1, blocking collectives, on_device(): lax.all_to_all(folded.astype(jnp.bfloat16), 'seq', split_axis=0, concat_a...  49.2 us
    all_gather x1, waiting for transfers between devices, on_device(): all_pre = lax.all_gather(pre_grad, 'seq', axis=0, tiled=True)  38 us
    all_to_all x1, blocking collectives, on_device(): lax.all_to_all(wide_rows, 'seq', split_axis=1, concat_axis=0, tiled=True)  26.4 us
    all_to_all x1, waiting for transfers between devices, on_device(): lax.all_to_all(part_cols.astype(jnp.bfloat16), 'seq', split_axis=0, conca...  20.1 us
    all_gather x1, blocking collectives, on_device(): lax.all_gather(part_rows, 'grp', axis=0).astype(jnp.float32)  13.6 us
    all_gather x1, blocking collectives, on_device(): lax.all_gather(outgoing.reshape(-1, llm_grad.shape[1]), 'grp', axis=1, ti...  10.7 us
    all_to_all x1, starting transfers between devices, on_device(): lax.all_to_all(part_cols.astype(jnp.bfloat16), 'seq', split_axis=0, conca...  6.43 us
  transfers between devices with their start and end apart: 4, of which 3 were waited for; matrix products, arithmetic and copies ran while one was open for 9% of the time, Pallas kernels for 0%

commit v1 on v0

--- a/solution.py
+++ b/solution.py
@@ -80,7 +80,15 @@
     recv_counts = jnp.sum(received * counts, 1)
     recv_widths = jnp.sum(received * widths, 1)
     wide_rows = lax.all_gather(outgoing.reshape(-1, llm_grad.shape[1]), "grp", axis=1, tiled=True)
-    sliced = lax.all_to_all(wide_rows, "seq", split_axis=1, concat_axis=0, tiled=True)
+    sliced = jnp.concatenate(
+        jax.lax.all_to_all(
+            jnp.stack(jnp.split(wide_rows, jax.lax.axis_size("seq"), 1), 0),
+            axis_name="seq",
+            split_axis=0,
+            concat_axis=0,
+        ),
+        axis=0,
+    )
     features = sliced.shape[1]
     by_owner = jnp.swapaxes(sliced.reshape(seq_count, seq_count, SLOT, features), 0, 1).reshape(
         -1, features

time: 298 us -> 298 us (level)
  no operation moved by 1% of the time
where the time goes in v1:
time: 298 us; the launch traced here: 297 us
  waiting for transfers between devices  124 us (42%)
  blocking collectives  99.9 us (34%)
  local copies, waits for them, and re-layouts  19.6 us (7%)
  matrix products  15.2 us (5%)
  between operations  14.4 us (5%)
  starting transfers between devices  12.2 us (4%)
  other arithmetic  11.3 us (4%)
    all_to_all x1, waiting for transfers between devices, on_device(): lax.all_to_all(weight_part.astype(jnp.bfloat16), 'seq', split_axis=0, con...  65.5 us
    all_to_all x1, blocking collectives, on_device(): lax.all_to_all(folded.astype(jnp.bfloat16), 'seq', split_axis=0, concat_a...  49.2 us
    all_gather x1, waiting for transfers between devices, on_device(): all_pre = lax.all_gather(pre_grad, 'seq', axis=0, tiled=True)  38 us
    all_to_all x1, blocking collectives, on_device(): jax.lax.all_to_all(jnp.stack(jnp.split(wide_rows, jax.lax.axis_size('seq'...  26.4 us
    all_to_all x1, waiting for transfers between devices, on_device(): lax.all_to_all(part_cols.astype(jnp.bfloat16), 'seq', split_axis=0, conca...  20.1 us
    all_gather x1, blocking collectives, on_device(): lax.all_gather(part_rows, 'grp', axis=0).astype(jnp.float32)  13.6 us
    all_gather x1, blocking collectives, on_device(): lax.all_gather(outgoing.reshape(-1, llm_grad.shape[1]), 'grp', axis=1, ti...  10.7 us
    all_to_all x1, starting transfers between devices, on_device(): lax.all_to_all(part_cols.astype(jnp.bfloat16), 'seq', split_axis=0, conca...  6.44 us
  transfers between devices with their start and end apart: 4, of which 3 were waited for; matrix products, arithmetic and copies ran while one was open for 9% of the time, Pallas kernels for 0%

profile of v1, /device:TPU:13, one launch (start us, length us, event | category | flops | bytes accessed | tf_op | source)
XLA Modules:
  0.0 296.8 jit_solution(16084033416917905342)
XLA Ops:
  7.2 0.9 reshape.486
  8.9 0.8 reshape.487
  10.4 0.8 gather_fusion
  11.3 10.7 %all_gather.15 = bf16[48,8192]{1,0:T(8,128)(2,1)S(1)} all-gather(bf16[48,4096]{1,0:T(8,128)(2,1)S(1)} %select_select_fusion), channel_id=1, replica_groups=mesh['grp'=2,'seq'=16] {'grp'}, dimensions={1}, use_global_device_ids=true | all-gather | bytes 1179648 | tf_op jit(solution)/shard_map/all_gather | solution.py:82
  22.2 26.4 %all_to_all.39 = bf16[16,48,512]{2,1,0:T(8,128)(2,1)S(1)} all-to-all(bf16[16,48,512]{2,1,0:T(8,128)(2,1)S(1)} %fusion.32), channel_id=1, replica_groups=mesh['grp'=2,'seq'=16] {'seq'}, dimensions={0} | all-to-all | bytes 1572864 | tf_op jit(solution)/shard_map/all_to_all | solution.py:84
  49.7 1.4 reshape.489
  51.1 2.7 convolution_convert_fusion.1
  53.9 49.2 %all_to_all.40 = bf16[16,48,1280]{2,1,0:T(8,128)(2,1)} all-to-all(bf16[16,48,1280]{2,1,0:T(8,128)(2,1)S(1)} %bitcast.141), channel_id=1, replica_groups=mesh['grp'=2,'seq'=16] {'seq'}, dimensions={0} | all-to-all | bytes 3932160 | tf_op jit(solution)/shard_map/all_to_all | solution.py:97
  103.1 1.9 reduce_sum.108
  105.0 0.8 fusion.26
  107.0 38.0 %all-gather.3.cloned.1.call-done = bf16[768,1280]{1,0:T(8,128)(2,1)} async-done(((bf16[48,1280]{1,0:T(8,128)(2,1)}), bf16[768,1280]{1,0:T(8,128)(2,1)}) %all-gather.3.cloned.1.call-update) | async-done | bytes 1966096 | tf_op jit(solution)/shard_map/all_gather | solution.py:105
  145.0 2.6 convolution_convert_fusion.2
  147.6 1.1 copy.20
  148.6 6.4 %all-to-all-start.2 = ((bf16[16,48,320]{2,1,0:T(8,128)(2,1)}), bf16[16,48,320]{2,1,0:T(8,128)(2,1)}, u32[]{:S(2)}, u32[]{:S(2)}) async-start(bf16[16,48,320]{2,1,0:T(8,128)(2,1)} %bitcast.28), calls=%async_computation.2 | async-start | bytes 1179648 | tf_op jit(solution)/shard_map/all_to_all | solution.py:107
  155.2 1.1 reshape.495
  156.7 20.1 %all-to-all-done.2 = bf16[16,48,320]{2,1,0:T(8,128)(2,1)} async-done(((bf16[16,48,320]{2,1,0:T(8,128)(2,1)}), bf16[16,48,320]{2,1,0:T(8,128)(2,1)}, u32[]{:S(2)}, u32[]{:S(2)}) %all-to-all-start.2) | async-done | bytes 491552 | tf_op jit(solution)/shard_map/all_to_all | solution.py:107
  176.8 2.0 copy.21
  178.8 2.3 all_gather.17
  181.1 13.6 %all_gather.18 = bf16[2,48,5120]{2,1,0:T(8,128)(2,1)S(1)} all-gather(bf16[1,48,5120]{2,1,0:T(8,128)(2,1)} %all_gather.17), channel_id=1, replica_groups=mesh['grp'=2,'seq'=16] {'grp'}, dimensions={0}, use_global_device_ids=true | all-gather | bytes 1474560 | tf_op jit(solution)/shard_map/all_gather | solution.py:110
  194.8 1.1 convert_reduce_fusion.1
  195.9 2.5 reshape.490
  198.4 2.4 multiply_reduce_fusion.1
  200.9 1.1 copy-done.1
  202.0 1.3 multiply_convert_fusion
  203.2 1.2 convert_element_type.82
  204.4 3.9 %convolution_convert_fusion = bf16[1280,1280]{1,0:T(8,128)(2,1)} fusion(bf16[192,1280]{1,0:T(8,128)(2,1)S(1)} %convert_element_type.82, bf16[192,1,1280]{2,0,1:T(8,128)(2,1)} %param.17), kind=kOutput, calls=%fused_computation.1 | convolution fusion | flops 632504320 | bytes 4259840 | tf_op jit(solution)/shard_map/dot_general | solution.py:139
  208.3 5.6 %all-to-all-start.3 = ((bf16[16,80,1280]{2,1,0:T(8,128)(2,1)}), bf16[16,80,1280]{2,1,0:T(8,128)(2,1)}, u32[]{:S(2)}, u32[]{:S(2)}) async-start(bf16[16,80,1280]{2,1,0:T(8,128)(2,1)} %bitcast.139), calls=%async_computation.3 | async-start | bytes 6553600 | tf_op jit(solution)/shard_map/all_to_all | solution.py:142
  214.0 1.1 reshape.491
  215.2 1.7 multiply_convert_fusion.1
  217.6 3.6 %fusion.1 = bf16[192,1,1280]{2,0,1:T(8,128)(2,1)} fusion(bf16[192,1280]{1,0:T(8,128)(2,1)S(1)} %multiply_convert_fusion.1, bf16[1280,1280]{1,0:T(8,128)(2,1)} %all-gather.5.cloned.1.call-done, bf16[192,1,1280]{2,0,1:T(8,128)(2,1)S(1)} %copy-done.6), kind=kOutput, calls=%fused_computation.6 | convolution fusion | flops 631848960 | bytes 4751360 | tf_op jit(solution)/shard_map/dot_general | solution.py:127
  221.2 65.5 %all-to-all-done.3 = bf16[16,80,1280]{2,1,0:T(8,128)(2,1)} async-done(((bf16[16,80,1280]{2,1,0:T(8,128)(2,1)}), bf16[16,80,1280]{2,1,0:T(8,128)(2,1)}, u32[]{:S(2)}, u32[]{:S(2)}) %all-to-all-start.3) | async-done | bytes 3276832 | tf_op jit(solution)/shard_map/all_to_all | solution.py:142
  286.7 3.2 %convert_reduce_fusion = f32[80,1280]{1,0:T(8,128)} fusion(bf16[16,80,1280]{2,1,0:T(8,128)(2,1)} %all-to-all-done.3), kind=kLoop, calls=%fused_computation.2 | loop fusion | flops 3174400 | bytes 3686400 | tf_op jit(solution)/shard_map/reduce_sum | solution.py:145
  (67 shorter events, 5.5 us)
Async XLA Ops:
  7.2 3.2 %copy-start = (bf16[256,4096]{1,0:T(8,128)(2,1)S(1)}, bf16[256,4096]{1,0:T(8,128)(2,1)}, u32[]{:S(2)}) copy-start(bf16[256,4096]{1,0:T(8,128)(2,1)} %param.11) | copy-start | bytes 6291460
  7.2 137.8 %all-gather.3.cloned.1.call-start = ((), (), s32[]{:S(2)}) async-start(), calls=%async_computation.4 | async-start | bytes 2088960 | tf_op jit(solution)/shard_map/all_gather | solution.py:105
  103.1 1.9 copy-start.4
  103.1 3.5 %copy-start.3 = (bf16[192,1,1280]{2,0,1:T(8,128)(2,1)S(1)}, bf16[192,1,1280]{2,0,1:T(8,128)(2,1)}, u32[]{:S(2)}) copy-start(bf16[192,1,1280]{2,0,1:T(8,128)(2,1)} %param.16) | copy-start | bytes 1474564
  105.8 111.8 %all-gather.5.cloned.1.call-start = ((), (), s32[]{:S(2)}) async-start(), calls=%async_computation.5 | async-start | bytes 3481600 | tf_op jit(solution)/shard_map/all_gather | solution.py:129
  148.6 28.2 %all-to-all-start.2 = ((bf16[16,48,320]{2,1,0:T(8,128)(2,1)}), bf16[16,48,320]{2,1,0:T(8,128)(2,1)}, u32[]{:S(2)}, u32[]{:S(2)}) async-start(bf16[16,48,320]{2,1,0:T(8,128)(2,1)} %bitcast.28), calls=%async_computation.2 | async-start | bytes 1179648 | tf_op jit(solution)/shard_map/all_to_all | solution.py:107
  195.9 2.6 copy-start.5
  200.9 1.1 copy-start.1
  208.3 5.7 %copy-start.2 = (f32[16,12,1280]{2,1,0:T(8,128)S(1)}, f32[16,12,1280]{2,1,0:T(8,128)}, u32[]{:S(2)}) copy-start(f32[16,12,1280]{2,1,0:T(8,128)} %copy-done.1) | copy-start | bytes 2949124
  208.3 78.4 %all-to-all-start.3 = ((bf16[16,80,1280]{2,1,0:T(8,128)(2,1)}), bf16[16,80,1280]{2,1,0:T(8,128)(2,1)}, u32[]{:S(2)}, u32[]{:S(2)}) async-start(bf16[16,80,1280]{2,1,0:T(8,128)(2,1)} %bitcast.139), calls=%async_computation.3 | async-start | bytes 6553600 | tf_op jit(solution)/shard_map/all_to_all | solution.py:142
  215.1 2.5 copy-start.6
Sparse Core Ops, SparseCore 0:
  105.9 39.0 all-gather.2
  147.3 52.0 all-gather.4
